TPU v7x, 32 devices: a whole 2x2x4 slice. The times are simulated.
32 devices in a mesh: dp: 32 (over z, y, x, core).
Axes of the slice: x: 2, y: 2, z: 4, core: 2. Of those that a mesh axis runs over, the one named last changes fastest.
Arguments:
- master: float32 [65536], P('dp'), may hold values from -6 to 6
- gradients: float32 [65536], P('dp'), may hold values from -6 to 6
- first_moment: float32 [65536], P('dp'), may hold values from -4 to 4
- second_moment: float32 [65536], P('dp'), may hold values from 0.01 to 1
- segment_ids: int32 [65536], P('dp'), may hold values from 0 to 63, as said below
- decay_mask: int32 [64], replicated, may hold values 0 or 1
Outputs:
- new_master: float32 [65536], P('dp')
- new_first: float32 [65536], P('dp')
- new_second: float32 [65536], P('dp')
- scaled_step: float32 [65536], P('dp')
- model_weights: bfloat16 [65536], replicated
Inputs may be any that keep to these rules, and one draw needn't show every extreme that they name: segment_ids never falls along the flat vector; each tensor 0 to 63 owns one contiguous run of 256 to 16384 elements, and one tensor has exactly 16384. `decay_mask`: each entry is 0 or 1.
All inputs are finite; a program needn't handle non-finite values.
Results may differ from a plain program's by a relative error of at most 0.0004.
Values may be sent and summed in bfloat16 or wider, within the bound.
A program may use at most 64 MiB of HBM per device.

v0:
```python
import math

import jax
import jax.numpy as jnp
from jax import lax
from jax.sharding import PartitionSpec as P

SEG_DEV = 2
STEP = 20


first_decay = 0.9
second_decay = 0.999
epsilon = 1e-06
weight_decay = 0.01
learn_rate = 0.006


def adam_direction(master, gradients, first_moment, second_moment, decay):
    new_first = first_decay * first_moment + (1.0 - first_decay) * gradients
    new_second = second_decay * second_moment + (1.0 - second_decay) * gradients * gradients
    hat_first = new_first / (1.0 - first_decay**STEP)
    hat_second = new_second / (1.0 - second_decay**STEP)
    direction = hat_first / (jnp.sqrt(hat_second) + epsilon) + weight_decay * decay * master
    return (new_first, new_second, direction)


def trust_ratio(weight_sq, step_sq):
    weight_norm = jnp.sqrt(weight_sq)
    step_norm = jnp.sqrt(step_sq)
    usable = (weight_norm > 0.0) & (step_norm > 0.0)
    return jnp.where(usable, weight_norm / jnp.where(usable, step_norm, 1.0), 1.0)


def block_rows(length):
    return math.gcd(length, 1024)


def one_hot_block(ids, width):
    columns = lax.broadcasted_iota(jnp.int32, (ids.shape[0], width), 1)
    return (ids[:, None] == columns).astype(jnp.float32)


def spread(table, ids, width):
    length = ids.shape[0]
    rows = block_rows(length)
    blocks = ids.reshape(length // rows, rows)

    def one_block(block_ids):
        return jnp.dot(one_hot_block(block_ids, width), table, precision=lax.Precision.HIGHEST)

    return lax.map(one_block, blocks).reshape(length, table.shape[1])


def collect(values, ids, width):
    length = ids.shape[0]
    rows = block_rows(length)
    blocks = ids.reshape(length // rows, rows)
    value_blocks = values.reshape(length // rows, rows, values.shape[1])

    def add_block(total, pair):
        block_ids, block_values = pair
        term = lax.dot_general(
            one_hot_block(block_ids, width),
            block_values,
            (((0,), (0,)), ((), ())),
            precision=lax.Precision.HIGHEST,
        )
        return (total + term, None)

    start = jnp.zeros((width, values.shape[1]), jnp.float32)
    total, unused = lax.scan(add_block, start, (blocks, value_blocks))
    return total


def to_global(partial_value, first_id, tensors, width):
    holder = jnp.zeros((tensors + width, partial_value.shape[1]), jnp.float32)
    placed = lax.dynamic_update_slice_in_dim(holder, partial_value, first_id, 0)
    return placed[:tensors]


def to_local(table, first_id, width, filler):
    padded = jnp.concatenate([table, jnp.full((width,), filler, jnp.float32)])
    return lax.dynamic_slice_in_dim(padded, first_id, width)


def shards(master, gradients, first_moment, second_moment, segment_ids, decay_mask):
    tensors = decay_mask.shape[0]
    width = 4 * SEG_DEV + 2
    first_id = segment_ids[0].astype(jnp.int32)
    local_ids = (segment_ids - first_id).astype(jnp.int32)
    local_mask = to_local(decay_mask.astype(jnp.float32), first_id, width, 0.0)
    decay = spread(local_mask[:, None], local_ids, width)[:, 0]
    weight_square = master * master
    new_first, new_second, direction = adam_direction(
        master, gradients, first_moment, second_moment, decay
    )
    stacked = jnp.stack([weight_square, direction * direction], axis=1)
    packed_partial = to_global(collect(stacked, local_ids, width), first_id, tensors, width)
    totals = lax.psum(packed_partial, "dp")
    ratios = to_local(trust_ratio(totals[:, 0], totals[:, 1]), first_id, width, 1.0)
    per_element = spread(ratios[:, None], local_ids, width)[:, 0]
    scaled_step = per_element * direction
    new_master = master - learn_rate * scaled_step
    model_weights = lax.all_gather(new_master.astype(jnp.bfloat16), "dp", axis=0, tiled=True)
    return (new_master, new_first, new_second, scaled_step, model_weights)


def solution(mesh):
    in_specs = (P("dp"), P("dp"), P("dp"), P("dp"), P("dp"), P())
    out_specs = (P("dp"), P("dp"), P("dp"), P("dp"), P())
    return jax.shard_map(shards, mesh=mesh, in_specs=in_specs, out_specs=out_specs, check_vma=False)
```

profile of v0, /device:TPU:0, one launch (start us, length us, event | category | flops | bytes accessed | tf_op | source)
XLA Modules:
  0.0 93.0 jit_solution(16898911853833414570)
XLA Ops:
  0.6 0.0 copy-start.4
  0.6 1.3 %slice.12 = s32[1]{0:T(128)} slice(s32[2048]{0:T(1024)} %param.16), slice={[0:1]} | slice | bytes 8 | tf_op jit(solution)/shard_map/slice | solution.py:90
  3.2 0.0 copy-start.5
  3.9 0.0 copy-done.5
  3.9 0.1 dynamic-slice_bitcast_fusion.1
  4.0 0.0 copy-done.4
  4.0 0.6 broadcast_subtract_fusion
  4.7 0.0 copy-start.2
  4.7 0.0 copy-start.3
  4.7 1.0 %while.31 = (s32[]{:T(128)}, f32[2,1024,1]{1,2,0:T(1,128)S(1)}, s32[2,1024]{1,0:T(2,128)S(1)}, f32[10,1]{0,1:T(1,128)S(1)}, s32[]{:T(128)}) while((s32[]{:T(128)}, f32[2,1024,1]{1,2,0:T(1,128)S(1)}, s32[2,1024]{1,0:T(2,128)S(1)}, f32[10,1]{0,1:T(1,128)S(1)}, s32[]{:T(128)}) %tuple.58), condition=%wide.region_1.2_spmd, body=%wide.region_0.1_spmd.sunk | while | flops 133122 | bytes 16973 | solution.py:52
  4.7 0.5 fusion.22
  5.2 0.5 fusion.22
  5.6 0.0 copy-start
  5.7 0.0 copy-start.1
  5.7 0.0 copy-done.2
  5.7 0.0 copy-done.3
  5.7 0.7 copy-done
  6.4 0.0 copy-done.1
  6.4 0.6 fusion.12
  7.0 0.8 while.33
  7.0 0.4 convolution_add_fusion.2
  7.5 0.4 convolution_add_fusion.2
  7.9 0.1 dynamic_update_slice.10
  8.0 42.0 %psum.7 = f32[64,2]{0,1:T(2,128)S(1)} all-reduce(f32[64,2]{0,1:T(2,128)S(1)} %bitcast.66), channel_id=1, replica_groups=mesh['dp'=32] {'dp'}, use_global_device_ids=true, to_apply=%region_4.5 | all-reduce | flops 128 | bytes 1024 | tf_op jit(solution)/shard_map/psum | solution.py:100
  50.1 0.1 dynamic-slice_bitcast_fusion
  50.1 0.9 %while.32 = (s32[]{:T(128)}, f32[2,1024,1]{1,2,0:T(1,128)S(1)}, s32[2,1024]{1,0:T(2,128)S(1)}, f32[10,1]{0,1:T(1,128)S(1)}, s32[]{:T(128)}) while((s32[]{:T(128)}, f32[2,1024,1]{1,2,0:T(1,128)S(1)}, s32[2,1024]{1,0:T(2,128)S(1)}, f32[10,1]{0,1:T(1,128)S(1)}, s32[]{:T(128)}) %tuple.70), condition=%wide.region_6.7_spmd, body=%wide.region_5.6_spmd.sunk | while | flops 133122 | bytes 16973 | solution.py:52
  50.2 0.5 fusion.24
  50.6 0.5 fusion.24
  51.1 0.6 fusion.11
  51.7 40.6 %all_gather.3 = bf16[65536]{0:T(1024)(128)(2,1)S(1)} all-gather(bf16[2048]{0:T(1024)(128)(2,1)S(1)} %get-tuple-element.113), channel_id=1, replica_groups=mesh['dp'=32] {'dp'}, dimensions={0}, use_global_device_ids=true | all-gather | bytes 135168 | tf_op jit(solution)/shard_map/all_gather | solution.py:105
  92.3 0.7 copy.35
  (15 shorter events, 0.1 us)
Async XLA Ops:
  0.6 3.3 %copy-start.4 = (s32[2048]{0:T(1024)S(1)}, s32[2048]{0:T(1024)}, u32[]{:S(2)}) copy-start(s32[2048]{0:T(1024)} %param.16) | copy-start | bytes 24580
  3.2 0.7 copy-start.5
  4.7 1.0 %copy-start.2 = (f32[2048]{0:T(1024)S(1)}, f32[2048]{0:T(1024)}, u32[]{:S(2)}) copy-start(f32[2048]{0:T(1024)} %param.14) | copy-start | bytes 24580
  4.7 1.0 %copy-start.3 = (f32[2048]{0:T(1024)S(1)}, f32[2048]{0:T(1024)}, u32[]{:S(2)}) copy-start(f32[2048]{0:T(1024)} %param.15) | copy-start | bytes 24580
  5.6 0.7 copy-start
  5.7 0.7 copy-start.1
where the time goes:
time: 93.4 us; the launch traced here: 93 us
  blocking collectives  82.6 us (88%)
  local copies, waits for them, and re-layouts  3.03 us (3%)
  between operations  2.73 us (3%)
  matrix products  2.58 us (3%)
  other arithmetic  1.93 us (2%)
    psum x1, blocking collectives, shards(): totals = lax.psum(packed_partial, 'dp')  42 us
    all_gather x1, blocking collectives, shards(): lax.all_gather(new_master.astype(jnp.bfloat16), 'dp', axis=0, tiled=True)  40.6 us

commit v1 on v0

v1 whole, which is shorter than its diff:
```python
import functools

import jax
import jax.numpy as jnp
from jax import lax
from jax.experimental import pallas as pl
from jax.experimental.pallas import tpu as pltpu
from jax.sharding import PartitionSpec as P

STEP = 20
LANES = 128
SHORTEST_RUN = 256
LONGEST_RUN = 16384

first_decay = 0.9
second_decay = 0.999
epsilon = 1e-06
weight_decay = 0.01
learn_rate = 0.006

MESH = pl.DeviceIdType.MESH


def total_of(values):
    return jnp.sum(jnp.sum(values, axis=0, keepdims=True), axis=1, keepdims=True)


def kernel(
    n,
    radius,
    local,
    master_hbm,
    gradients_hbm,
    first_hbm,
    second_hbm,
    ids_hbm,
    mask_hbm,
    new_master_hbm,
    new_first_hbm,
    new_second_hbm,
    scaled_hbm,
    weights_hbm,
    inputs,
    ids_vmem,
    edge_ids,
    mask_smem,
    outputs,
    weights_vmem,
    to_right,
    to_left,
    received,
    load_sem,
    store_sem,
    near_send,
    near_recv,
    far_send,
    far_recv,
):
    me = lax.axis_index("dp")
    rows = master_hbm.shape[0]
    tensors = mask_hbm.shape[0]

    received[...] = jnp.zeros_like(received)
    barrier = pltpu.get_barrier_semaphore()
    for distance in range(1, n):
        pl.semaphore_signal(
            barrier, inc=1, device_id=(lax.rem(me + distance, n),), device_id_type=MESH
        )

    loads = [
        pltpu.make_async_copy(source, target, load_sem.at[position])
        for position, (source, target) in enumerate(
            [
                (ids_hbm.at[pl.ds(0, 1)], edge_ids.at[pl.ds(0, 1)]),
                (ids_hbm.at[pl.ds(rows - 1, 1)], edge_ids.at[pl.ds(1, 1)]),
                (mask_hbm, mask_smem),
                (ids_hbm, ids_vmem),
                (first_hbm, inputs.at[2]),
                (gradients_hbm, inputs.at[1]),
                (second_hbm, inputs.at[3]),
                (master_hbm, inputs.at[0]),
            ]
        )
    ]
    for load in loads:
        load.start()
    for load in loads:
        load.wait()

    first_id = edge_ids[0, 0]
    last_id = edge_ids[1, LANES - 1]
    ids = ids_vmem[...]
    is_last = ids == last_id
    inside = [ids == first_id + k for k in range(local)]
    decay = jnp.zeros(ids.shape, jnp.float32)
    for k in range(local):
        entry = mask_smem[jnp.minimum(first_id + k, tensors - 1)].astype(jnp.float32)
        decay = jnp.where(inside[k], entry, decay)

    master = inputs[0]
    gradients = inputs[1]
    new_first = first_decay * inputs[2] + (1.0 - first_decay) * gradients
    new_second = second_decay * inputs[3] + (1.0 - second_decay) * gradients * gradients
    hat_first = new_first / (1.0 - first_decay**STEP)
    hat_second = new_second / (1.0 - second_decay**STEP)
    direction = hat_first / (jnp.sqrt(hat_second) + epsilon) + weight_decay * decay * master
    weight_square = master * master
    step_square = direction * direction

    def sums(chosen):
        return (
            total_of(jnp.where(chosen, weight_square, 0.0)),
            total_of(jnp.where(chosen, step_square, 0.0)),
        )

    weight_first, step_first = sums(inside[0])
    weight_last, step_last = sums(is_last)
    lane = lax.broadcasted_iota(jnp.int32, (1, LANES), 1)

    def message(segment, weight, step):
        return jnp.where(
            lane == 0, segment.astype(jnp.float32), jnp.where(lane == 1, weight, step)
        )

    to_right[...] = message(last_id, weight_last, step_last)
    to_left[...] = message(first_id, weight_first, step_first)
    outputs[1] = new_first
    outputs[2] = new_second

    pl.semaphore_wait(barrier, n - 1)

    def near_copy(source, slot, target):
        return pltpu.make_async_remote_copy(
            src_ref=source,
            dst_ref=received.at[pl.ds(slot, 1)],
            send_sem=near_send.at[slot],
            recv_sem=near_recv.at[slot],
            device_id=(target,),
            device_id_type=MESH,
        )

    for distance in range(radius, 0, -1):

        @pl.when(me + distance < n)
        def _():
            near_copy(to_right, distance - 1, me + distance).start()

        @pl.when(me >= distance)
        def _():
            near_copy(to_left, radius + distance - 1, me - distance).start()

    stores = [
        pltpu.make_async_copy(outputs.at[1], new_first_hbm, store_sem.at[0]),
        pltpu.make_async_copy(outputs.at[2], new_second_hbm, store_sem.at[1]),
    ]
    for store in stores:
        store.start()

    middle = [sums(inside[k]) for k in range(1, local)]

    for distance in range(1, radius + 1):

        @pl.when(me >= distance)
        def _():
            near_copy(to_right, distance - 1, me - distance).wait_recv()

        @pl.when(me + distance < n)
        def _():
            near_copy(to_left, radius + distance - 1, me + distance).wait_recv()

    table = received[...]
    segment_column = table[:, 0:1]

    def gathered(segment):
        found = jnp.where(segment_column == segment.astype(jnp.float32), table, 0.0)
        found = jnp.sum(found, axis=0, keepdims=True)
        return found[:, 1:2], found[:, 2:3]

    weight_more, step_more = gathered(first_id)
    weight_sq = jnp.broadcast_to(weight_first + weight_more, ids.shape)
    step_sq = jnp.broadcast_to(step_first + step_more, ids.shape)
    for k in range(1, local):
        weight_sq = jnp.where(inside[k], middle[k - 1][0], weight_sq)
        step_sq = jnp.where(inside[k], middle[k - 1][1], step_sq)
    weight_more, step_more = gathered(last_id)
    weight_sq = jnp.where(is_last, weight_last + weight_more, weight_sq)
    step_sq = jnp.where(is_last, step_last + step_more, step_sq)

    weight_norm = jnp.sqrt(weight_sq)
    step_norm = jnp.sqrt(step_sq)
    usable = (weight_norm > 0.0) & (step_norm > 0.0)
    trust = jnp.where(usable, weight_norm / jnp.where(usable, step_norm, 1.0), 1.0)
    scaled_step = trust * direction
    new_master = master - learn_rate * scaled_step
    weights_vmem[...] = new_master.astype(jnp.bfloat16)
    outputs[3] = scaled_step
    outputs[0] = new_master

    mine = weights_hbm.at[pl.ds(pl.multiple_of(me * rows, rows), rows)]

    def far_copy(distance):
        return pltpu.make_async_remote_copy(
            src_ref=weights_vmem,
            dst_ref=mine,
            send_sem=far_send.at[distance - 1],
            recv_sem=far_recv.at[distance - 1],
            device_id=(lax.rem(me + distance, n),),
            device_id_type=MESH,
        )

    for distance in range(1, n):
        far_copy(distance).start()
    for position, (source, target) in enumerate(
        [
            (weights_vmem, mine),
            (outputs.at[3], scaled_hbm),
            (outputs.at[0], new_master_hbm),
        ]
    ):
        store = pltpu.make_async_copy(source, target, store_sem.at[2 + position])
        store.start()
        stores.append(store)

    for distance in range(1, radius + 1):

        @pl.when(me + distance < n)
        def _():
            near_copy(to_right, distance - 1, me + distance).wait_send()

        @pl.when(me >= distance)
        def _():
            near_copy(to_left, radius + distance - 1, me - distance).wait_send()

    for store in stores:
        store.wait()
    for distance in range(1, n):
        far_copy(distance).wait_send()
    for distance in range(1, n):
        far_copy(distance).wait_recv()


def solution(mesh):
    n = mesh.shape["dp"]

    def shards(master, gradients, first_moment, second_moment, segment_ids, decay_mask):
        length = master.shape[0]
        rows = length // LANES
        tensors = decay_mask.shape[0]
        radius = min(n - 1, (LONGEST_RUN - 2) // length + 1)
        local = min(tensors, (length - 2) // SHORTEST_RUN + 2)
        block = jax.ShapeDtypeStruct((rows, LANES), jnp.float32)
        flat = [
            x.reshape(rows, LANES)
            for x in (master, gradients, first_moment, second_moment, segment_ids)
        ]
        anywhere = pl.BlockSpec(memory_space=pl.ANY)
        outs = pl.pallas_call(
            functools.partial(kernel, n, radius, local),
            out_shape=(block,) * 4 + (jax.ShapeDtypeStruct((n * rows, LANES), jnp.bfloat16),),
            in_specs=[anywhere] * 6,
            out_specs=(anywhere,) * 5,
            scratch_shapes=[
                pltpu.VMEM((4, rows, LANES), jnp.float32),
                pltpu.VMEM((rows, LANES), jnp.int32),
                pltpu.SMEM((2, LANES), jnp.int32),
                pltpu.SMEM((tensors,), jnp.int32),
                pltpu.VMEM((4, rows, LANES), jnp.float32),
                pltpu.VMEM((rows, LANES), jnp.bfloat16),
                pltpu.VMEM((1, LANES), jnp.float32),
                pltpu.VMEM((1, LANES), jnp.float32),
                pltpu.VMEM((2 * radius, LANES), jnp.float32),
                pltpu.SemaphoreType.DMA((8,)),
                pltpu.SemaphoreType.DMA((5,)),
                pltpu.SemaphoreType.DMA((2 * radius,)),
                pltpu.SemaphoreType.DMA((2 * radius,)),
                pltpu.SemaphoreType.DMA((n - 1,)),
                pltpu.SemaphoreType.DMA((n - 1,)),
            ],
            compiler_params=pltpu.CompilerParams(collective_id=0, has_side_effects=True),
        )(*flat, decay_mask)
        return tuple(x.reshape(-1) for x in outs)

    in_specs = (P("dp"), P("dp"), P("dp"), P("dp"), P("dp"), P())
    out_specs = (P("dp"), P("dp"), P("dp"), P("dp"), P())
    return jax.shard_map(shards, mesh=mesh, in_specs=in_specs, out_specs=out_specs, check_vma=False)
```

time: 93.4 us -> 22 us (0.24)
  blocking collectives: 82.6 us -> 0 us
  Pallas kernels: 0 us -> 16 us
  matrix products: 2.58 us -> 0 us
  between operations: 2.73 us -> 0.65 us
  local copies, waits for them, and re-layouts: 3.03 us -> 4.96 us
  other arithmetic: 1.93 us -> 0 us
    psum x1 -> x0, blocking collectives: 42 us -> none  [shards(): totals = lax.psum(packed_partial, 'dp')]
    all_gather x1 -> x0, blocking collectives: 40.6 us -> none  [shards(): lax.all_gather(new_master.astype(jnp.bfloat16), 'dp', axis=0, tiled=True)]
    pallas_call x0 -> x1, Pallas kernels: none -> 16 us  [shards(): pl.pallas_call(functools.partial(kernel, n, radius, local), out_shape=(bl...]
    unnamed x13, local copies, waits for them, and re-layouts: 1.37 us -> 4.96 us
    dot_general x6 -> x0, matrix products: 2.58 us -> none  [the longest x4 1.81 us: one_block(): jnp.dot(one_hot_block(block_ids, width), table, precision=lax.Precision.H...]
    slice x1 -> x0, local copies, waits for them, and re-layouts: 1.26 us -> none  [shards(): first_id = segment_ids[0].astype(jnp.int32)]
where the time goes in v1:
time: 22 us; the launch traced here: 21.6 us
  Pallas kernels  16 us (73%)
  local copies, waits for them, and re-layouts  4.96 us (23%)
  between operations  0.65 us (3%)
    pallas_call x1, Pallas kernels, shards(): pl.pallas_call(functools.partial(kernel, n, radius, local), out_shape=(bl...  16 us
    unnamed x13, local copies, waits for them, and re-layouts  4.96 us

profile of v1, /device:TPU:0, one launch (start us, length us, event | category | flops | bytes accessed | tf_op | source)
XLA Modules:
  0.0 21.6 jit_solution(15486935272892339589)
XLA Ops:
  0.6 16.0 %shard_map.101 = (f32[16,128]{1,0:T(8,128)}, f32[16,128]{1,0:T(8,128)}, f32[16,128]{1,0:T(8,128)}, f32[16,128]{1,0:T(8,128)}, bf16[512,128]{1,0:T(8,128)(2,1)}) custom-call(f32[16,128]{1,0:T(8,128)} %bitcast.15, f32[16,128]{1,0:T(8,128)} %bitcast.16, f32[16,128]{1,0:T(8,128)} %bitcast.17, f32[16,128]{1,0:T(8,128)} %bitcast.18, s32[16,128]{1,0:T(8,128)} %bitcast.19, ...), custom_call_target="tpu_custom_call" | custom-call | tf_op jit(solution)/shard_map/pallas_call | solution.py:257
  16.6 0.0 copy-start.3
  16.6 0.7 %copy-done.3 = f32[16,128]{1,0:T(8,128)S(1)} copy-done((f32[16,128]{1,0:T(8,128)S(1)}, f32[16,128]{1,0:T(8,128)}, u32[]{:S(2)}) %copy-start.3) | copy-done | bytes 8216
  17.3 0.0 copy-start.2
  17.3 0.6 %copy.16 = f32[2048]{0:T(1024)} copy(f32[2048]{0:T(1024)S(1)} %bitcast.14) | data formatting | bytes 16384
  17.9 0.1 copy-done.2
  18.0 0.0 copy-start.1
  18.0 0.6 %copy.17 = f32[2048]{0:T(1024)} copy(f32[2048]{0:T(1024)S(1)} %bitcast.13) | data formatting | bytes 16384
  18.6 0.1 copy-done.1
  18.7 0.0 copy-start
  18.7 0.6 %copy.18 = f32[2048]{0:T(1024)} copy(f32[2048]{0:T(1024)S(1)} %bitcast.12) | data formatting | bytes 16384
  19.3 0.1 copy-done
  19.4 0.6 %copy.19 = f32[2048]{0:T(1024)} copy(f32[2048]{0:T(1024)S(1)} %bitcast.11) | data formatting | bytes 16384
  20.0 1.6 %copy.20 = bf16[65536]{0:T(1024)(128)(2,1)} copy(bf16[65536]{0:T(1024)(128)(2,1)} %bitcast.10) | data formatting | bytes 262144
Async XLA Ops:
  16.6 0.7 %copy-start.3 = (f32[16,128]{1,0:T(8,128)S(1)}, f32[16,128]{1,0:T(8,128)}, u32[]{:S(2)}) copy-start(f32[16,128]{1,0:T(8,128)} %get-tuple-element.10) | copy-start | bytes 24580
  17.3 0.7 %copy-start.2 = (f32[16,128]{1,0:T(8,128)S(1)}, f32[16,128]{1,0:T(8,128)}, u32[]{:S(2)}) copy-start(f32[16,128]{1,0:T(8,128)} %get-tuple-element.11) | copy-start | bytes 24580
  18.0 0.7 %copy-start.1 = (f32[16,128]{1,0:T(8,128)S(1)}, f32[16,128]{1,0:T(8,128)}, u32[]{:S(2)}) copy-start(f32[16,128]{1,0:T(8,128)} %get-tuple-element.12) | copy-start | bytes 24580
  18.7 0.7 %copy-start = (f32[16,128]{1,0:T(8,128)S(1)}, f32[16,128]{1,0:T(8,128)}, u32[]{:S(2)}) copy-start(f32[16,128]{1,0:T(8,128)} %get-tuple-element.13) | copy-start | bytes 24580
